TPU v7x, 64 devices: a 2x2x8 block of a 4x4x8 slice. The times are simulated.
64 devices in a mesh: rep: 4 (over x, y), data: 16 (over z, core).
Axes of the slice: x: 2, y: 2, z: 8, core: 2. Of those that a mesh axis runs over, the one named last changes fastest.
The devices are a block of a 4x4x8 slice.
Arguments:
- x: bfloat16 [4096, 4096], P(('rep', 'data')), parts along dimension 0
- adapter_id: int32 [4096], P(('rep', 'data')), parts along dimension 0
- w_gate: bfloat16 [4096, 14336], replicated
- w_up: bfloat16 [4096, 14336], replicated
- w_down: bfloat16 [14336, 4096], replicated
- a_gate: bfloat16 [256, 8, 4096], P('data')
- b_gate: bfloat16 [256, 8, 14336], P('data')
- a_up: bfloat16 [256, 8, 4096], P('data')
- b_up: bfloat16 [256, 8, 14336], P('data')
- a_down: bfloat16 [256, 8, 14336], P('data')
- b_down: bfloat16 [256, 8, 4096], P('data')
Outputs:
- output: bfloat16 [4096, 4096], P(('rep', 'data')), parts along dimension 0
There are 4 independent parts. A program takes and returns all parts, laid end to end along the dimension named above; an argument that names none is the same for every part.
All inputs are finite; a program needn't handle non-finite values.
Results may differ from a plain program's by a relative error of at most 0.00571077.
Values are sent between devices in bfloat16 or wider.
A program may use at most 768 MiB of HBM per device.

v0:
```python
import jax
import jax.numpy as jnp
from jax import lax
from jax.sharding import PartitionSpec as P, NamedSharding

value_a10 = 32


def value_a9(tok_rows, row_ids, a_mat, b_mat):
    array_b10 = value_a10 / a_mat.shape[1]
    a_rows = jnp.take(a_mat, row_ids, axis=0)
    b_rows = jnp.take(b_mat, row_ids, axis=0)
    low_rank = jnp.einsum("md,mrd->mr", tok_rows, a_rows, preferred_element_type=jnp.float32).astype(jnp.bfloat16)
    full_rows = jnp.einsum("ns,nsg->ng", low_rank, b_rows, preferred_element_type=jnp.float32)
    return (array_b10 * full_rows).astype(jnp.bfloat16)


def solution(mesh):
    groups = mesh.shape["data"]
    row_spec = P(("rep", "data"), None)
    id_spec = P(("rep", "data"))
    owned_spec = P("data", None, None)

    def device_step(x, adapter_id, w_gate, w_up, w_down, a_gate, b_gate, a_up, b_up, a_down, b_down):
        tok_count = x.shape[0]
        per_owner = a_gate.shape[0]
        capacity = (3 * tok_count + groups - 1) // groups
        owner_idx = adapter_id // per_owner
        local_ad = adapter_id % per_owner
        owner_hot = (owner_idx[:, None] == jnp.arange(groups)[None, :]).astype(jnp.int32)
        arrival = jnp.sum(jnp.cumsum(owner_hot, axis=0) * owner_hot, axis=1) - 1
        slot_idx = owner_idx * capacity + arrival
        slot_hot = (slot_idx[:, None] == jnp.arange(groups * capacity)[None, :]).astype(jnp.int32)
        dispatch = slot_hot.astype(jnp.bfloat16)
        send_ids = jnp.sum(slot_hot * local_ad[:, None], axis=0)
        send_x = jnp.einsum("tm,td->md", dispatch, x, preferred_element_type=jnp.float32).astype(jnp.bfloat16)
        recv_ids = lax.all_to_all(send_ids, "data", 0, 0, tiled=True)
        recv_x = lax.all_to_all(send_x, "data", 0, 0, tiled=True)
        gate_back = lax.all_to_all(value_a9(recv_x, recv_ids, a_gate, b_gate), "data", 0, 0, tiled=True)
        up_back = lax.all_to_all(value_a9(recv_x, recv_ids, a_up, b_up), "data", 0, 0, tiled=True)
        gate_pre = jnp.dot(x, w_gate, preferred_element_type=jnp.float32) + jnp.einsum("tm,mf->tf", dispatch, gate_back, preferred_element_type=jnp.float32)
        up_pre = jnp.dot(x, w_up, preferred_element_type=jnp.float32) + jnp.einsum("tm,mf->tf", dispatch, up_back, preferred_element_type=jnp.float32)
        hidden = (jax.nn.silu(gate_pre) * up_pre).astype(jnp.bfloat16)
        send_h = jnp.einsum("tm,tf->mf", dispatch, hidden, preferred_element_type=jnp.float32).astype(jnp.bfloat16)
        recv_h = lax.all_to_all(send_h, "data", 0, 0, tiled=True)
        down_back = lax.all_to_all(value_a9(recv_h, recv_ids, a_down, b_down), "data", 0, 0, tiled=True)
        down_out = jnp.dot(hidden, w_down, preferred_element_type=jnp.float32) + jnp.einsum("tm,md->td", dispatch, down_back, preferred_element_type=jnp.float32)
        return (x.astype(jnp.float32) + down_out).astype(jnp.bfloat16)

    return jax.shard_map(device_step, mesh=mesh, in_specs=(row_spec, id_spec, P(), P(), P(), owned_spec, owned_spec, owned_spec, owned_spec, owned_spec, owned_spec), out_specs=row_spec, check_vma=False)
```

profile of v0, /device:TPU:21, one launch (start us, length us, event | category | flops | bytes accessed | tf_op | source)
XLA Modules:
  0.0 887.3 jit_solution(17201778950455627023)
XLA Ops:
  0.0 0.0 copy-start
  0.0 0.8 and_select_fusion.1
  0.8 0.1 fusion.41
  0.8 0.1 reduce_window_sum.11
  0.9 0.2 select_reduce_fusion.1
  1.1 0.0 copy-start.5
  1.1 0.1 select_reduce_fusion
  1.2 0.7 all_to_all.51
  1.9 10.7 %all-to-all-start.1 = ((s32[16,12,1]{1,2,0:T(1,128)}), s32[16,12,1]{1,2,0:T(1,128)S(1)}, u32[]{:S(2)}, u32[]{:S(2)}) async-start(s32[16,12,1]{1,2,0:T(1,128)} %bitcast), calls=%async_computation.1 | async-start | bytes 16384 | tf_op jit(solution)/shard_map/all_to_all | solution.py:37
  12.7 1.7 convolution_convert_fusion.1
  14.4 1.5 all_to_all.48
  15.9 3.7 all-to-all-done.1
  19.5 0.0 copy-done.5
  19.5 4.2 all-to-all-start
  23.7 0.5 broadcast.74
  24.2 0.7 reduce.3
  24.9 0.1 all_to_all.53
  25.0 0.0 copy-done
  25.0 7.8 gather_fusion
  32.8 18.8 %gather_fusion.1 = bf16[192,8,14336]{2,1,0:T(8,128)(2,1)} fusion(bf16[16,8,14336]{2,1,0:T(8,128)(2,1)} %param.21, s32[1024]{0:T(1024)S(1)} %pad_clamp_fusion), kind=kCustom, calls=%fused_computation.1.clone | custom fusion | bytes 88081152 | tf_op jit(solution)/shard_map/jit(_take)/gather | solution.py:12
  51.6 21.5 %all-to-all-done = bf16[16,12,4096]{2,1,0:T(8,128)(2,1)S(1)} async-done(((bf16[16,12,4096]{2,1,0:T(8,128)(2,1)}), bf16[16,12,4096]{2,1,0:T(8,128)(2,1)S(1)}, u32[]{:S(2)}, u32[]{:S(2)}) %all-to-all-start) | async-done | bytes 1572896 | tf_op jit(solution)/shard_map/all_to_all | solution.py:38
  73.2 4.4 reshape.103
  77.5 12.5 %fusion.18 = f32[192,1,8]{2,1,0:T(1,128)S(1)} fusion(bf16[192,4096,1]{1,2,0:T(2,128)(2,1)} %reshape.103, bf16[192,8,4096]{2,1,0:T(8,128)(2,1)} %gather_fusion, pred[192]{0:T(512)(128)(4,1)S(1)} %compare_and_fusion), kind=kOutput, calls=%fused_computation.27 | convolution fusion | flops 18874368 | bytes 14162112 | tf_op jit(solution)/shard_map/md,mrd->mr/dot_general | solution.py:13
  90.1 22.2 %fusion.4 = f32[192,1,14336]{2,1,0:T(1,128)} fusion(bf16[192,8,14336]{2,1,0:T(8,128)(2,1)} %gather_fusion.1, pred[192]{0:T(512)(128)(4,1)S(1)} %compare_and_fusion, bf16[192,8,1]{1,0,2:T(8,128)(2,1)S(1)} %convert_bitcast_fusion.2), kind=kOutput, calls=%fused_computation.10 | convolution fusion | flops 66060288 | bytes 55053504 | tf_op jit(solution)/shard_map/ns,nsg->ng/dot_general | solution.py:14
  112.3 9.7 %fusion.24 = bf16[192,14336]{1,0:T(8,128)(2,1)} fusion(f32[192,1,14336]{2,1,0:T(1,128)} %fusion.4), kind=kLoop, calls=%fused_computation.35 | loop fusion | flops 5505024 | bytes 16515072 | tf_op jit(solution)/shard_map/convert_element_type | solution.py:15
  122.0 8.1 all_to_all.54
  130.2 5.1 all-to-all-start.2
  135.3 0.0 copy-done.2
  135.3 7.8 gather_fusion.2
  143.1 18.8 %gather_fusion.3 = bf16[192,8,14336]{2,1,0:T(8,128)(2,1)} fusion(bf16[16,8,14336]{2,1,0:T(8,128)(2,1)} %param.23, s32[1024]{0:T(1024)S(1)} %pad_clamp_fusion), kind=kCustom, calls=%fused_computation.4.clone | custom fusion | bytes 88081152 | tf_op jit(solution)/shard_map/jit(_take)/gather | solution.py:12
  161.9 12.5 %fusion.16 = f32[192,1,8]{2,1,0:T(1,128)S(1)} fusion(bf16[192,4096,1]{1,2,0:T(2,128)(2,1)} %reshape.103, bf16[192,8,4096]{2,1,0:T(8,128)(2,1)} %gather_fusion.2, pred[192]{0:T(512)(128)(4,1)S(1)} %compare_and_fusion), kind=kOutput, calls=%fused_computation.25 | convolution fusion | flops 18874368 | bytes 14162112 | tf_op jit(solution)/shard_map/md,mrd->mr/dot_general | solution.py:13
  174.4 21.9 %fusion.2 = f32[192,1,14336]{2,1,0:T(1,128)} fusion(bf16[192,8,14336]{2,1,0:T(8,128)(2,1)} %gather_fusion.3, pred[192]{0:T(512)(128)(4,1)S(1)} %compare_and_fusion, bf16[192,8,1]{1,0,2:T(8,128)(2,1)S(1)} %convert_bitcast_fusion.1), kind=kOutput, calls=%fused_computation.8 | convolution fusion | flops 66060288 | bytes 55053504 | tf_op jit(solution)/shard_map/ns,nsg->ng/dot_general | solution.py:14
  196.3 9.8 %fusion.23 = bf16[192,14336]{1,0:T(8,128)(2,1)} fusion(f32[192,1,14336]{2,1,0:T(1,128)} %fusion.2), kind=kLoop, calls=%fused_computation.33 | loop fusion | flops 5505024 | bytes 16515072 | tf_op jit(solution)/shard_map/convert_element_type | solution.py:15
  206.1 8.1 all_to_all.57
  214.1 86.4 %all-to-all-done.2 = bf16[16,12,14336]{2,1,0:T(8,128)(2,1)} async-done(((bf16[16,12,14336]{2,1,0:T(8,128)(2,1)}), bf16[16,12,14336]{2,1,0:T(8,128)(2,1)}, u32[]{:S(2)}, u32[]{:S(2)}) %all-to-all-start.2) | async-done | bytes 5505056 | tf_op jit(solution)/shard_map/all_to_all | solution.py:39
  300.5 8.3 all-to-all-start.3
  308.9 8.3 all_to_all.56
  317.2 0.0 copy-done.6
  317.2 5.6 fusion.35
  322.8 151.3 %all-to-all-done.3 = bf16[16,12,14336]{2,1,0:T(8,128)(2,1)} async-done(((bf16[16,12,14336]{2,1,0:T(8,128)(2,1)}), bf16[16,12,14336]{2,1,0:T(8,128)(2,1)}, u32[]{:S(2)}, u32[]{:S(2)}) %all-to-all-start.3) | async-done | bytes 5505056 | tf_op jit(solution)/shard_map/all_to_all | solution.py:40
  474.1 8.3 all_to_all.59
  482.5 5.6 fusion.34
  488.1 0.0 copy-done.4
  488.1 40.6 %convolution_add_fusion.1 = f32[64,14336]{1,0:T(8,128)} fusion(f32[64,14336]{1,0:T(8,128)} %fusion.35, bf16[64,4096]{1,0:T(8,128)(2,1)S(1)} %copy-done.4, bf16[4096,14336]{1,0:T(8,128)(2,1)} %param.17), kind=kOutput, calls=%fused_computation.20 | convolution fusion | flops 7517110272 | bytes 125304832 | tf_op jit(solution)/shard_map/dot_general | solution.py:41
  528.7 41.8 %fusion.13 = bf16[64,14336]{1,0:T(8,128)(2,1)S(1)} fusion(f32[64,14336]{1,0:T(8,128)} %fusion.34, bf16[64,4096]{1,0:T(8,128)(2,1)S(1)} %copy-done.4, bf16[4096,14336]{1,0:T(8,128)(2,1)} %param.18, f32[64,14336]{1,0:T(8,128)} %convolution_add_fusion.1), kind=kOutput, calls=%fused_computation.22 | convolution fusion | flops 7522615296 | bytes 127139840 | tf_op jit(solution)/shard_map/dot_general | solution.py:42
  570.5 4.1 convolution_convert_fusion
  574.6 7.9 all_to_all.60
  582.6 8.7 all-to-all-start.4
  591.3 0.0 copy-start.3
  591.3 18.9 %gather_fusion.4 = bf16[192,8,14336]{2,1,0:T(8,128)(2,1)} fusion(bf16[16,8,14336]{2,1,0:T(8,128)(2,1)} %param.24, s32[1024]{0:T(1024)S(1)} %pad_clamp_fusion), kind=kCustom, calls=%fused_computation.5.clone | custom fusion | bytes 88081152 | tf_op jit(solution)/shard_map/jit(_take)/gather | solution.py:11
  610.2 7.8 gather_fusion.5
  618.0 138.2 %all-to-all-done.4 = bf16[16,12,14336]{2,1,0:T(8,128)(2,1)} async-done(((bf16[16,12,14336]{2,1,0:T(8,128)(2,1)}), bf16[16,12,14336]{2,1,0:T(8,128)(2,1)}, u32[]{:S(2)}, u32[]{:S(2)}) %all-to-all-start.4) | async-done | bytes 5505056 | tf_op jit(solution)/shard_map/all_to_all | solution.py:45
  756.2 15.9 %reshape.105 = bf16[192,14336,1]{1,2,0:T(2,128)(2,1)} reshape(bf16[16,12,14336]{2,1,0:T(8,128)(2,1)} %all-to-all-done.4) | data formatting | bytes 11010048 | tf_op jit(solution)/shard_map/all_to_all | solution.py:45
  772.1 39.6 %fusion = f32[192,1,8]{2,1,0:T(1,128)S(1)} fusion(bf16[192,14336,1]{1,2,0:T(2,128)(2,1)} %reshape.105, bf16[192,8,14336]{2,1,0:T(8,128)(2,1)} %gather_fusion.4, pred[192]{0:T(512)(128)(4,1)S(1)} %compare_and_fusion), kind=kOutput, calls=%fused_computation.6 | convolution fusion | flops 66060288 | bytes 49551552 | tf_op jit(solution)/shard_map/md,mrd->mr/dot_general | solution.py:13
  811.7 6.6 fusion.14
  818.3 2.9 fusion.30
  821.3 3.4 all_to_all.63
  824.7 8.8 all-to-all-start.5
  833.5 0.0 copy-start.1
  833.5 40.1 %fusion.48 = f32[64,4096]{1,0:T(8,128)} fusion(bf16[64,14336]{1,0:T(8,128)(2,1)S(1)} %fusion.13, bf16[14336,4096]{1,0:T(8,128)(2,1)} %param.19), kind=kOutput, calls=%fused_computation.79 | convolution fusion | flops 7516192768 | bytes 120324096 | tf_op jit(solution)/shard_map/dot_general | solution.py:47
  873.6 8.3 all-to-all-done.5
  882.0 2.5 all_to_all.65
  884.4 2.5 fusion.29
  886.9 0.0 copy-done.1
  (11 shorter events, 0.1 us)
Async XLA Ops:
  0.0 25.0 %copy-start = (bf16[16,8,4096]{2,1,0:T(8,128)(2,1)S(1)}, bf16[16,8,4096]{2,1,0:T(8,128)(2,1)}, u32[]{:S(2)}) copy-start(bf16[16,8,4096]{2,1,0:T(8,128)(2,1)} %param.20) | copy-start | bytes 3145732
  1.1 18.4 %copy-start.5 = (s32[64]{0:T(128)}, s32[64]{0:T(128)S(1)}, u32[]{:S(2)}) copy-start(s32[64]{0:T(128)S(1)} %add_add_fusion) | copy-start | bytes 772
  1.9 17.6 %all-to-all-start.1 = ((s32[16,12,1]{1,2,0:T(1,128)}), s32[16,12,1]{1,2,0:T(1,128)S(1)}, u32[]{:S(2)}, u32[]{:S(2)}) async-start(s32[16,12,1]{1,2,0:T(1,128)} %bitcast), calls=%async_computation.1 | async-start | bytes 16384 | tf_op jit(solution)/shard_map/all_to_all | solution.py:37
  19.5 53.6 %all-to-all-start = ((bf16[16,12,4096]{2,1,0:T(8,128)(2,1)}), bf16[16,12,4096]{2,1,0:T(8,128)(2,1)S(1)}, u32[]{:S(2)}, u32[]{:S(2)}) async-start(bf16[16,12,4096]{2,1,0:T(8,128)(2,1)} %all_to_all.48), calls=%async_computation | async-start | bytes 4194304 | tf_op jit(solution)/shard_map/all_to_all | solution.py:38
  122.0 13.2 %copy-start.2 = (bf16[16,8,4096]{2,1,0:T(8,128)(2,1)S(1)}, bf16[16,8,4096]{2,1,0:T(8,128)(2,1)}, u32[]{:S(2)}) copy-start(bf16[16,8,4096]{2,1,0:T(8,128)(2,1)} %param.22) | copy-start | bytes 3145732
  130.2 170.4 %all-to-all-start.2 = ((bf16[16,12,14336]{2,1,0:T(8,128)(2,1)}), bf16[16,12,14336]{2,1,0:T(8,128)(2,1)}, u32[]{:S(2)}, u32[]{:S(2)}) async-start(bf16[16,12,14336]{2,1,0:T(8,128)(2,1)} %all_to_all.54), calls=%async_computation.2 | async-start | bytes 14680064 | tf_op jit(solution)/shard_map/all_to_all | solution.py:39
  214.1 103.0 %copy-start.6 = (s32[64]{0:T(128)S(1)}, s32[64]{0:T(128)}, u32[]{:S(2)}) copy-start(s32[64]{0:T(128)} %copy-done.5) | copy-start | bytes 772
  300.5 173.6 %all-to-all-start.3 = ((bf16[16,12,14336]{2,1,0:T(8,128)(2,1)}), bf16[16,12,14336]{2,1,0:T(8,128)(2,1)}, u32[]{:S(2)}, u32[]{:S(2)}) async-start(bf16[16,12,14336]{2,1,0:T(8,128)(2,1)} %all_to_all.57), calls=%async_computation.3 | async-start | bytes 14680064 | tf_op jit(solution)/shard_map/all_to_all | solution.py:40
  322.8 165.3 %copy-start.4 = (bf16[64,4096]{1,0:T(8,128)(2,1)S(1)}, bf16[64,4096]{1,0:T(8,128)(2,1)}, u32[]{:S(2)}) copy-start(bf16[64,4096]{1,0:T(8,128)(2,1)} %param.15) | copy-start | bytes 1572868
  582.6 173.6 %all-to-all-start.4 = ((bf16[16,12,14336]{2,1,0:T(8,128)(2,1)}), bf16[16,12,14336]{2,1,0:T(8,128)(2,1)}, u32[]{:S(2)}, u32[]{:S(2)}) async-start(bf16[16,12,14336]{2,1,0:T(8,128)(2,1)} %all_to_all.60), calls=%async_computation.4 | async-start | bytes 14680064 | tf_op jit(solution)/shard_map/all_to_all | solution.py:45
  591.3 18.9 %copy-start.3 = (bf16[16,8,4096]{2,1,0:T(8,128)(2,1)S(1)}, bf16[16,8,4096]{2,1,0:T(8,128)(2,1)}, u32[]{:S(2)}) copy-start(bf16[16,8,4096]{2,1,0:T(8,128)(2,1)} %param.25) | copy-start | bytes 3145732
  824.7 57.3 %all-to-all-start.5 = ((bf16[16,12,4096]{2,1,0:T(8,128)(2,1)}), bf16[16,12,4096]{2,1,0:T(8,128)(2,1)}, u32[]{:S(2)}, u32[]{:S(2)}) async-start(bf16[16,12,4096]{2,1,0:T(8,128)(2,1)} %all_to_all.63), calls=%async_computation.5 | async-start | bytes 4194304 | tf_op jit(solution)/shard_map/all_to_all | solution.py:46
  833.5 53.4 %copy-start.1 = (bf16[16,8,4096]{2,1,0:T(8,128)(2,1)S(1)}, bf16[16,8,4096]{2,1,0:T(8,128)(2,1)}, u32[]{:S(2)}) copy-start(bf16[16,8,4096]{2,1,0:T(8,128)(2,1)} %param.20) | copy-start | bytes 3145732
where the time goes:
time: 897 us; the launch traced here: 887 us
  waiting for transfers between devices  409 us (46%)
  matrix products  257 us (29%)
  local copies, waits for them, and re-layouts  150 us (17%)
  starting transfers between devices  45.9 us (5%)
  other arithmetic  24.4 us (3%)
    all_to_all x1, waiting for transfers between devices, device_step(): lax.all_to_all(value_a9(recv_x, recv_ids, a_up, b_up), 'data', 0, 0, tile...  151 us
    all_to_all x1, waiting for transfers between devices, device_step(): recv_h = lax.all_to_all(send_h, 'data', 0, 0, tiled=True)  138 us
    all_to_all x1, waiting for transfers between devices, device_step(): lax.all_to_all(value_a9(recv_x, recv_ids, a_gate, b_gate), 'data', 0, 0,...  86.4 us
    dot_general x3, matrix products, value_a9(): jnp.einsum('md,mrd->mr', tok_rows, a_rows, preferred_element_type=jnp.flo...  64.6 us
    dot_general x3, matrix products, value_a9(): jnp.einsum('ns,nsg->ng', low_rank, b_rows, preferred_element_type=jnp.flo...  50.7 us
    gather x3, local copies, waits for them, and re-layouts, value_a9(): b_rows = jnp.take(b_mat, row_ids, axis=0)  45.4 us
    dot_general x1, matrix products, device_step(): jnp.dot(x, w_up, preferred_element_type=jnp.float32)  41.8 us
    dot_general x1, matrix products, device_step(): jnp.dot(x, w_gate, preferred_element_type=jnp.float32)  40.6 us
  transfers between devices with their start and end apart: 6, of which 6 were waited for; matrix products, arithmetic and copies ran while one was open for 19% of the time, Pallas kernels for 0%

commit v1 on v0

v1 whole, which is shorter than its diff:
```python
import functools

import jax
import jax.numpy as jnp
from jax import lax
from jax.experimental import pallas as pl
from jax.experimental.pallas import tpu as pltpu
from jax.sharding import PartitionSpec as P

ALPHA = 32
MESH = pl.DeviceIdType.MESH
BF16, F32 = jnp.bfloat16, jnp.float32
SUB = 512
LANES = 128
PACK = 4
HELD = 9
SLOTS = 24
AHEAD = 3


def nt_dot(a, b):
    return lax.dot_general(a, b, (((1,), (1,)), ((), ())), preferred_element_type=F32)


def dot(a, b):
    return jnp.dot(a, b, preferred_element_type=F32)


def layer_kernel(
    groups, cap, scale, per_owner, rank,
    x_hbm, ids_ref, wg_hbm, wu_hbm, wd_hbm, ag_hbm, bg_hbm, au_hbm, bu_hbm, ad_hbm, bd_hbm,
    out_hbm,
    x_own, send, mask_send, recv, mask_recv, xs, acc, hid, wbuf, abuf, lbuf, bdbuf,
    low, lowm, lowd, oacc, back_send, back_recv, out_own, pick,
    w_sem, misc_sem, a_sem, l_sem, xs_send, xs_recv, m_send, m_recv, b_send, b_recv, o_sem,
):
    tok, width = x_own.shape
    rows = groups * cap
    wide = wg_hbm.shape[1]
    ranks = per_owner * rank
    tile = 2 * SUB
    n_chunk = width // SUB
    n_tile = wide // tile
    n_out = width // SUB
    per_msg = cap // PACK
    blocks = SUB // LANES
    n_step1 = n_chunk * n_tile
    n_step2 = n_out * n_tile
    n_block = 2 * n_step1 + n_step2

    me = lax.axis_index("data")
    peers = [2 * (groups // 4) + k for k in (0, 1)]
    order = []
    for d in range(groups // 4, 0, -1):
        order += [2 * d, 2 * d + 1, groups - 2 * d, groups - 2 * d + 1]
    seen = []
    for off in order + list(range(groups)):
        off = off % groups
        if off and off not in seen:
            seen.append(off)
    peers = [lax.rem(me + off, groups) for off in seen]

    def w_copies(b):
        slot = lax.rem(b, SLOTS)
        return slot

    def start_w1(step, b):
        early = step < HELD * n_chunk
        late = step - HELD * n_chunk
        c = jnp.where(early, step // HELD, lax.rem(late, n_chunk))
        n = jnp.where(early, lax.rem(step, HELD), HELD + late // n_chunk)
        k0 = pl.multiple_of(c * SUB, SUB)
        n0 = pl.multiple_of(n * tile, tile)
        for which, w in enumerate((wg_hbm, wu_hbm)):
            slot = lax.rem(b + which, SLOTS)
            for half in range(2):
                pltpu.make_async_copy(
                    w.at[pl.ds(k0, SUB), pl.ds(n0 + half * SUB, SUB)], wbuf.at[slot, half], w_sem.at[slot]
                ).start()

    def start_w2(step, b):
        j = step // n_tile
        k = lax.rem(step, n_tile)
        slot = lax.rem(b, SLOTS)
        n0 = pl.multiple_of(j * SUB, SUB)
        for half in range(2):
            k0 = pl.multiple_of(k * tile + half * SUB, SUB)
            pltpu.make_async_copy(
                wd_hbm.at[pl.ds(k0, SUB), pl.ds(n0, SUB)], wbuf.at[slot, half], w_sem.at[slot]
            ).start()

    def wait_w(slot):
        pltpu.make_async_copy(wbuf.at[slot], wbuf.at[slot], w_sem.at[slot]).wait()

    def l_copies(n):
        s = lax.rem(n, 2)
        n0 = pl.multiple_of(n * tile, tile)
        return [
            pltpu.make_async_copy(src.at[:, pl.ds(n0, tile)], lbuf.at[s, i], l_sem.at[s])
            for i, src in enumerate((bg_hbm, bu_hbm, ad_hbm))
        ]

    x_copy = pltpu.make_async_copy(x_hbm, x_own, misc_sem.at[0])
    bd_copy = pltpu.make_async_copy(bd_hbm, bdbuf, misc_sem.at[1])
    x_copy.start()
    for i in range(2):
        for c in range(n_chunk):
            src = (ag_hbm, au_hbm)[i]
            pltpu.make_async_copy(
                src.at[:, pl.ds(c * SUB, SUB)], abuf.at[c, pl.ds(i * ranks, ranks)], a_sem.at[c]
            ).start()

    @pl.loop(0, SLOTS // 2)
    def _(s):
        start_w1(s, 2 * s)

    bd_copy.start()
    for n in range(2):
        for cp in l_copies(n):
            cp.start()

    barrier = pltpu.get_barrier_semaphore()
    for peer in peers:
        pl.semaphore_signal(barrier, inc=1, device_id={"data": peer}, device_id_type=MESH)

    ids = ids_ref[...].astype(F32)
    r0 = lax.broadcasted_iota(jnp.int32, (tok, tok), 0).astype(F32)
    r1 = lax.broadcasted_iota(jnp.int32, (tok, tok), 1).astype(F32)
    ids_row = jnp.broadcast_to(ids, (tok, tok))
    ids_col = jnp.broadcast_to(jnp.sum(jnp.where(r0 == r1, ids_row, 0.0), axis=1, keepdims=True), (tok, tok))
    own_row = jnp.floor((ids_row + 0.5) * (1.0 / per_owner))
    own_col = jnp.floor((ids_col + 0.5) * (1.0 / per_owner))
    same = own_row == own_col
    arr_row = jnp.sum(jnp.where(same & (r0 < r1), 1.0, 0.0), axis=0, keepdims=True)
    arr_col = jnp.sum(jnp.where(same & (r1 < r0), 1.0, 0.0), axis=1, keepdims=True)
    slot_row = own_row[:1, :] * cap + arr_row
    slot_col = own_col[:, :1] * cap + arr_col
    loc_col = ids_col[:, :1] - own_col[:, :1] * per_owner
    s_row = lax.broadcasted_iota(jnp.int32, (rows, tok), 0).astype(F32)
    spread = jnp.where(s_row == jnp.broadcast_to(slot_row, (rows, tok)), 1.0, 0.0).astype(BF16)
    s_col = lax.broadcasted_iota(jnp.int32, (tok, rows), 1).astype(F32)
    pick[...] = jnp.where(s_col == jnp.broadcast_to(slot_col, (tok, rows)), 1.0, 0.0).astype(BF16)
    lane = lax.broadcasted_iota(jnp.int32, (tok, ranks), 1).astype(F32)
    lane_ad = jnp.floor((lane + 0.5) * (1.0 / rank))
    mine = jnp.where(lane_ad == jnp.broadcast_to(loc_col, (tok, ranks)), 1.0, 0.0).astype(BF16)

    low[...] = jnp.zeros_like(low)
    lowd[...] = jnp.zeros_like(lowd)
    oacc[...] = jnp.zeros_like(oacc)

    mask_send[...] = dot(spread, mine).astype(BF16).reshape(mask_send.shape)
    x_copy.wait()
    for c in range(n_chunk):
        part = dot(spread, x_own[:, c * SUB:(c + 1) * SUB]).astype(BF16)
        for q in range(blocks):
            send[:, c * blocks + q] = part[:, q * LANES:(q + 1) * LANES].reshape(groups, per_msg, PACK, LANES)

    mine_at = pl.ds(per_msg * me, per_msg)

    def send_x(c):
        for peer in peers:
            pltpu.make_async_remote_copy(
                src_ref=send.at[peer, pl.ds(c * blocks, blocks)],
                dst_ref=recv.at[pl.ds(c * blocks, blocks), mine_at],
                send_sem=xs_send.at[c], recv_sem=xs_recv.at[c],
                device_id={"data": peer}, device_id_type=MESH,
            ).start()

    def send_out(j):
        for peer in peers:
            pltpu.make_async_remote_copy(
                src_ref=back_send.at[peer, pl.ds(j * blocks, blocks)],
                dst_ref=back_recv.at[pl.ds(j * blocks, blocks), mine_at],
                send_sem=b_send.at[j], recv_sem=b_recv.at[j],
                device_id={"data": peer}, device_id_type=MESH,
            ).start()

    def await_peers(buf, c, sem):
        view = buf.at[pl.ds(c * blocks, blocks), pl.ds(0, per_msg * (groups - 1))]
        pltpu.make_async_copy(view, view, sem).wait()

    def await_sent(buf, c, sem):
        view = buf.at[pl.ds(0, groups - 1), pl.ds(c * blocks, blocks)]
        pltpu.make_async_copy(view, view, sem).wait()

    @pl.loop(0, n_chunk * blocks)
    def _(q):
        recv[q, mine_at] = send[me, q]

    mask_recv[mine_at] = mask_send[mine_at]

    pl.semaphore_wait(barrier, groups - 1)

    @pl.loop(0, AHEAD)
    def _(c):
        send_x(c)

    @pl.loop(0, HELD)
    def _(n):
        acc[0, n] = jnp.zeros(acc.shape[2:], F32)
        acc[1, n] = jnp.zeros(acc.shape[2:], F32)

    def arrive(c):
        @pl.when(c + AHEAD < n_chunk)
        def _():
            send_x(c + AHEAD)

        @pl.when(c == n_chunk - AHEAD)
        def _():
            for peer in peers:
                pltpu.make_async_remote_copy(
                    src_ref=mask_send.at[pl.ds(per_msg * peer, per_msg)],
                    dst_ref=mask_recv.at[mine_at],
                    send_sem=m_send, recv_sem=m_recv,
                    device_id={"data": peer}, device_id_type=MESH,
                ).start()

        await_peers(recv, c, xs_recv.at[c])
        for q in range(blocks):
            xs[c, :, q * LANES:(q + 1) * LANES] = recv[c * blocks + q].reshape(rows, LANES)
        pltpu.make_async_copy(abuf.at[c], abuf.at[c], a_sem.at[c]).wait()
        low[...] += nt_dot(xs[c], abuf[c])

        @pl.when(c == n_chunk - 1)
        def _():
            view = mask_recv.at[pl.ds(0, per_msg * (groups - 1))]
            pltpu.make_async_copy(view, view, m_recv).wait()
            mask = mask_recv[...].reshape(rows, ranks).astype(F32) > 0.0
            for i in range(2):
                kept = low[:, i * ranks:(i + 1) * ranks].astype(BF16).astype(F32)
                lowm[i] = jnp.where(mask, kept, 0.0).astype(BF16)

    def delta(a, b):
        return (scale * dot(a, b)).astype(BF16).astype(F32)

    @pl.loop(0, n_step1)
    def _(step):
        early = step < HELD * n_chunk
        late = step - HELD * n_chunk
        c = jnp.where(early, step // HELD, lax.rem(late, n_chunk))
        n = jnp.where(early, lax.rem(step, HELD), HELD + late // n_chunk)
        a = lax.rem(n, HELD)

        @pl.when(early & (n == 0))
        def _():
            arrive(c)

        for which in range(2):
            slot = lax.rem(2 * step + which, SLOTS)
            wait_w(slot)
            for half in range(2):
                cols = slice(half * SUB, (half + 1) * SUB)
                acc[which, a, :, cols] += dot(xs[c], wbuf[slot, half])

        nxt = 2 * step + SLOTS

        @pl.when(nxt < 2 * n_step1)
        def _():
            start_w1(step + SLOTS // 2, nxt)

        @pl.when(nxt >= 2 * n_step1)
        def _():
            start_w2(nxt - 2 * n_step1, nxt)
            start_w2(nxt + 1 - 2 * n_step1, nxt + 1)

        @pl.when(c == n_chunk - 1)
        def _():
            s = lax.rem(n, 2)
            pltpu.make_async_copy(lbuf.at[s], lbuf.at[s], l_sem.at[s]).wait()
            piece = tile // 4
            for p in range(4):
                cols = slice(p * piece, (p + 1) * piece)
                g = acc[0, a, :, cols] + delta(lowm[0], lbuf[s, 0, :, cols])
                u = acc[1, a, :, cols] + delta(lowm[1], lbuf[s, 1, :, cols])
                hid[n, :, cols] = (jax.nn.silu(g) * u).astype(BF16)
            acc[0, a] = jnp.zeros(acc.shape[2:], F32)
            acc[1, a] = jnp.zeros(acc.shape[2:], F32)
            lowd[...] += nt_dot(hid[n], lbuf[s, 2])

            @pl.when(n + 2 < n_tile)
            def _():
                for cp in l_copies(n + 2):
                    cp.start()

    mask = mask_recv[...].reshape(rows, ranks).astype(F32) > 0.0
    lowm[0] = jnp.where(mask, lowd[...].astype(BF16).astype(F32), 0.0).astype(BF16)
    bd_copy.wait()

    def combine(j):
        await_peers(back_recv, j, b_recv.at[j])
        part = jnp.concatenate([back_recv[j * blocks + q].reshape(rows, LANES) for q in range(blocks)], axis=1)
        o0 = pl.multiple_of(j * SUB, SUB)
        out_own[j] = dot(pick[...], part).astype(BF16)
        pltpu.make_async_copy(out_own.at[j], out_hbm.at[:, pl.ds(o0, SUB)], o_sem).start()

    @pl.loop(0, n_step2)
    def _(step):
        j = step // n_tile
        k = lax.rem(step, n_tile)
        b = 2 * n_step1 + step
        slot = lax.rem(b, SLOTS)
        wait_w(slot)
        for half in range(2):
            oacc[...] += dot(hid[k, :, half * SUB:(half + 1) * SUB], wbuf[slot, half])

        @pl.when(b + SLOTS < n_block)
        def _():
            start_w2(step + SLOTS, b + SLOTS)

        @pl.when((k == 1) & (j > 0))
        def _():
            send_out(j - 1)

        @pl.when((k == n_tile - 2) & (j > 1))
        def _():
            combine(j - 2)

        @pl.when(k == n_tile - 1)
        def _():
            o0 = pl.multiple_of(j * SUB, SUB)
            total = xs[j].astype(F32) + (oacc[...] + delta(lowm[0], bdbuf[:, pl.ds(o0, SUB)]))
            oacc[...] = jnp.zeros_like(oacc)
            row = total.astype(BF16)
            for q in range(blocks):
                back_send[:, j * blocks + q] = row[:, q * LANES:(q + 1) * LANES].reshape(
                    groups, per_msg, PACK, LANES)
            for q in range(blocks):
                back_recv[j * blocks + q, mine_at] = back_send[me, j * blocks + q]

    send_out(n_out - 1)
    combine(n_out - 2)
    combine(n_out - 1)

    for c in range(n_chunk):
        await_sent(send, c, xs_send.at[c])
    view = mask_send.at[pl.ds(0, per_msg * (groups - 1))]
    pltpu.make_async_copy(view, view, m_send).wait()
    for j in range(n_out):
        await_sent(back_send, j, b_send.at[j])
    pltpu.make_async_copy(out_own, out_own, o_sem).wait()


def solution(mesh):
    groups = mesh.shape["data"]
    row_spec = P(("rep", "data"), None)
    id_spec = P(("rep", "data"))
    owned_spec = P("data", None, None)

    def device_step(x, adapter_id, w_gate, w_up, w_down, a_gate, b_gate, a_up, b_up, a_down, b_down):
        tok, width = x.shape
        wide = w_gate.shape[1]
        per_owner, rank = a_gate.shape[:2]
        cap = (3 * tok + groups - 1) // groups
        rows, ranks, tile = groups * cap, per_owner * rank, 2 * SUB
        per_msg, n_chunk, n_tile = cap // PACK, width // SUB, wide // tile
        assert cap % PACK == 0 and width % SUB == 0 and wide % tile == 0 and ranks == LANES

        def flat(m):
            return m.reshape(ranks, m.shape[2])

        vm = pltpu.VMEM
        any_spec = pl.BlockSpec(memory_space=pl.ANY)
        msg = (groups, width // LANES, per_msg, PACK, LANES)
        got = (width // LANES, groups * per_msg, PACK, LANES)
        small = (groups * per_msg, PACK, LANES)
        dma = pltpu.SemaphoreType.DMA
        return pl.pallas_call(
            functools.partial(layer_kernel, groups, cap, ALPHA / rank, per_owner, rank),
            out_shape=jax.ShapeDtypeStruct((tok, width), BF16),
            in_specs=[any_spec, pl.BlockSpec(memory_space=pltpu.VMEM)] + [any_spec] * 9,
            out_specs=any_spec,
            scratch_shapes=[
                vm((tok, width), BF16), vm(msg, BF16), vm(small, BF16), vm(got, BF16), vm(small, BF16),
                vm((n_chunk, rows, SUB), BF16), vm((2, HELD, rows, tile), F32), vm((n_tile, rows, tile), BF16),
                vm((SLOTS, 2, SUB, SUB), BF16), vm((n_chunk, 2 * ranks, SUB), BF16), vm((2, 3, ranks, tile), BF16),
                vm((ranks, width), BF16), vm((rows, 2 * ranks), F32), vm((2, rows, ranks), BF16),
                vm((rows, ranks), F32), vm((rows, SUB), F32), vm(msg, BF16), vm(got, BF16),
                vm((width // SUB, tok, SUB), BF16), vm((tok, rows), BF16),
                dma((SLOTS,)), dma((2,)), dma((n_chunk,)), dma((2,)), dma((n_chunk,)), dma((n_chunk,)), dma, dma,
                dma((width // SUB,)), dma((width // SUB,)), dma,
            ],
            compiler_params=pltpu.CompilerParams(
                collective_id=0, has_side_effects=True, vmem_limit_bytes=67043328),
            name="owner_layer",
        )(x, adapter_id.reshape(1, tok), w_gate, w_up, w_down, flat(a_gate), flat(b_gate), flat(a_up), flat(b_up),
          flat(a_down), flat(b_down))

    return jax.shard_map(
        device_step, mesh=mesh,
        in_specs=(row_spec, id_spec, P(), P(), P()) + (owned_spec,) * 6,
        out_specs=row_spec, check_vma=False)
```

time: 897 us -> 183 us (0.20); the launches traced: 887 us -> 183 us
  waiting for transfers between devices: 409 us -> 0 us
  matrix products: 257 us -> 0 us
  Pallas kernels: 0 us -> 181 us
  local copies, waits for them, and re-layouts: 150 us -> 1.87 us
  starting transfers between devices: 45.9 us -> 0 us
  other arithmetic: 24.4 us -> 0 us
    all_to_all x6 -> x0, waiting for transfers between devices: 409 us -> none  [the longest x1 151 us: device_step(): lax.all_to_all(value_a9(recv_x, recv_ids, a_up, b_up), 'data', 0, 0, tile...]
    dot_general x14 -> x0, matrix products: 257 us -> none  [the longest x3 64.6 us: value_a9(): jnp.einsum('md,mrd->mr', tok_rows, a_rows, preferred_element_type=jnp.flo...]
    pallas_call x0 -> x1, Pallas kernels: none -> 181 us  [device_step(): pl.pallas_call(functools.partial(layer_kernel, groups, cap, ALPHA / rank,...]
    gather x6 -> x0, local copies, waits for them, and re-layouts: 79.9 us -> none  [the longest x3 45.4 us: value_a9(): b_rows = jnp.take(b_mat, row_ids, axis=0)]
    all_to_all x13 -> x0, local copies, waits for them, and re-layouts: 69.7 us -> none  [the longest x2 23.9 us: device_step(): recv_h = lax.all_to_all(send_h, 'data', 0, 0, tiled=True)]
    all_to_all x6 -> x0, starting transfers between devices: 45.9 us -> none  [the longest x1 10.7 us: device_step(): recv_ids = lax.all_to_all(send_ids, 'data', 0, 0, tiled=True)]
    convert_element_type x7 -> x0, other arithmetic: 22.5 us -> none  [the longest x3 22.4 us: value_a9(): return (array_b10 * full_rows).astype(jnp.bfloat16)]
  transfers between devices with their start and end apart: 6 -> 0, of which waited for: 6 -> 0; matrix products, arithmetic and copies ran while one was open for 19% -> 0% of each run, Pallas kernels for 0% -> 0%
where the time goes in v1:
time: 183 us
  Pallas kernels  181 us (99%)
  local copies, waits for them, and re-layouts  1.87 us (1%)
    pallas_call x1, Pallas kernels, device_step(): pl.pallas_call(functools.partial(layer_kernel, groups, cap, ALPHA / rank,...  181 us

profile of v1, /device:TPU:21, one launch (start us, length us, event | category | flops | bytes accessed | tf_op | source)
XLA Modules:
  0.0 182.7 jit_solution(3346183942111416219)
XLA Ops:
  0.0 180.9 %owner_layer.1 = bf16[64,4096]{1,0:T(8,128)(2,1)} custom-call(bf16[64,4096]{1,0:T(8,128)(2,1)} %x_hbm.1, s32[1,64]{1,0:T(1,128)} %bitcast.13, bf16[4096,14336]{1,0:T(8,128)(2,1)} %wg_hbm.1, bf16[4096,14336]{1,0:T(8,128)(2,1)} %wu_hbm.1, bf16[14336,4096]{1,0:T(8,128)(2,1)} %wd_hbm.1, bf16[128,4096]{1,0:T(8,128)(2,1)} %bitcast.10, bf16[128,14336]{1,0:T(8,128)(2,1)} %bitcast.7, ...), custom_call_target="tpu_custom_call" | custom-call | tf_op jit(solution)/shard_map/owner_layer/pallas_call | solution.py:367
  180.9 1.9 %copy.13 = bf16[64,4096]{1,0:T(8,128)(2,1)} copy(bf16[64,4096]{1,0:T(8,128)(2,1)} %owner_layer.1) | data formatting | bytes 1048576

commit v2 on v1

v2 whole, which is shorter than its diff:
```python
import functools

import jax
import jax.numpy as jnp
from jax import lax
from jax.experimental import pallas as pl
from jax.experimental.pallas import tpu as pltpu
from jax.sharding import PartitionSpec as P

ALPHA = 32
MESH = pl.DeviceIdType.MESH
BF16, F32 = jnp.bfloat16, jnp.float32
SUB = 512
LANES = 128
PACK = 4
HELD = 9
PAIRS = 12
LBUFS = 4


def nt_dot(a, b):
    return lax.dot_general(a, b, (((1,), (1,)), ((), ())), preferred_element_type=F32)


def dot(a, b):
    return jnp.dot(a, b, preferred_element_type=F32)


def layer_kernel(
    groups, cap, scale, per_owner, rank,
    x_hbm, ids_ref, wg_hbm, wu_hbm, wd_hbm, ag_hbm, bg_hbm, au_hbm, bu_hbm, ad_hbm, bd_hbm,
    out_hbm,
    x_own, send, mask_send, recv, mask_recv, xs, acc, hid, wbuf, abuf, lbuf, bdbuf,
    low, lowm, lowd, oacc, back_send, back_recv, out_own, pick,
    w_sem, misc_sem, a_sem, l_sem, xs_send, xs_recv, m_send, m_recv, b_send, b_recv, o_sem,
):
    tok, width = x_own.shape
    rows = groups * cap
    wide = wg_hbm.shape[1]
    ranks = per_owner * rank
    n_chunk = width // SUB
    n_tile = wide // SUB
    n_out = width // SUB
    per_msg = cap // PACK
    blocks = SUB // LANES
    n_held = 2 * HELD
    k_pair = 4 * SUB
    n_kp = wide // k_pair
    n_deep = n_chunk // 2
    messages = [(0, 1), (1, 1)] + [(c, 2) for c in range(2, n_chunk, 2)]

    me = lax.axis_index("data")
    seen = []
    for d in range(groups // 4, 0, -1):
        for off in (2 * d, 2 * d + 1, groups - 2 * d, groups - 2 * d + 1):
            if off % groups and off % groups not in seen:
                seen.append(off % groups)
    seen += [off for off in range(1, groups) if off not in seen]
    peers = [lax.rem(me + off, groups) for off in seen]

    def nxt(slot):
        return jnp.where(slot == PAIRS - 1, 0, slot + 1)

    def start_a1(slot, c, n):
        for which, w in enumerate((wg_hbm, wu_hbm)):
            for half in range(2):
                n0 = pl.multiple_of(n * (2 * SUB) + half * SUB, SUB)
                pltpu.make_async_copy(
                    w.at[pl.ds(c * SUB, SUB), pl.ds(n0, SUB)],
                    wbuf.at[slot, which, pl.ds(half * SUB, SUB)], w_sem.at[slot],
                ).start()

    def start_gu(slot, p, n):
        k0 = pl.multiple_of(p * (2 * SUB), 2 * SUB)
        n0 = pl.multiple_of(n * SUB, SUB)
        for which, w in enumerate((wg_hbm, wu_hbm)):
            pltpu.make_async_copy(
                w.at[pl.ds(k0, 2 * SUB), pl.ds(n0, SUB)], wbuf.at[slot, which], w_sem.at[slot]).start()

    def start_d(slot, j, kp):
        n0 = pl.multiple_of(j * SUB, SUB)
        for half in range(2):
            k0 = pl.multiple_of(kp * k_pair + half * 2 * SUB, 2 * SUB)
            pltpu.make_async_copy(
                wd_hbm.at[pl.ds(k0, 2 * SUB), pl.ds(n0, SUB)], wbuf.at[slot, half], w_sem.at[slot]).start()

    def wait_w(slot):
        pltpu.make_async_copy(wbuf.at[slot], wbuf.at[slot], w_sem.at[slot]).wait()

    def issue(i, slot):
        for count, start in (
            (2 * HELD, lambda i: start_a1(slot, i // HELD, i % HELD)),
            ((n_deep - 1) * n_held, lambda i: start_gu(slot, 1 + i // n_held, i % n_held)),
            ((n_tile - n_held) * n_deep, lambda i: start_gu(slot, i % n_deep, n_held + i // n_deep)),
            (n_out * n_kp, lambda i: start_d(slot, i // n_kp, i % n_kp)),
        ):
            if i < count:
                start(i)
                return
            i -= count

    kinds = []
    for o in range(2):
        kinds += [("a1", o, n) for n in range(HELD)]
    for o in range(1, n_deep):
        kinds += [("gu", o, n) for n in range(n_held)]
    for n in range(n_held, n_tile):
        kinds += [("gu", o, n) for o in range(n_deep)]
    for o in range(n_out):
        kinds += [("d", o, n) for n in range(n_kp)]
    starts = {"a1": start_a1, "gu": start_gu, "d": start_d}
    n_pair = len(kinds)

    def run(first, count, size, body):
        step = 0
        while step < count:
            def refill(s):
                return [kinds[q] if q < n_pair else None for q in
                        range(first + s * size + PAIRS, first + (s + 1) * size + PAIRS)]

            def rule(a, b):
                if any((p is None) != (q is None) or (p and p[0] != q[0]) for p, q in zip(a, b)):
                    return None
                return [p and (q[1] - p[1], q[2] - p[2]) for p, q in zip(a, b)]

            end = step + 1
            delta = None
            while end < count:
                d = rule(refill(end - 1), refill(end))
                if d is None or (delta is not None and d != delta):
                    break
                delta = d
                end += 1
            base = refill(step)
            slot0 = (first + step * size) % PAIRS

            def one(s, slot, base=base, delta=delta, step=step):
                slots = [slot]
                for _ in range(size - 1):
                    slots.append(nxt(slots[-1]))
                body(s, slots)
                for i, item in enumerate(base):
                    if item is None:
                        continue
                    kind, o, n = item
                    if delta is not None:
                        o, n = o + (s - step) * delta[i][0], n + (s - step) * delta[i][1]
                    starts[kind](slots[i], o, n)
                return nxt(slots[-1])

            if end - step == 1:
                one(step, slot0)
            else:
                lax.fori_loop(step, end, one, jnp.int32(slot0))
            step = end

    def l_copies(n, s):
        n0 = pl.multiple_of(n * SUB, SUB)
        return [
            pltpu.make_async_copy(src.at[:, pl.ds(n0, SUB)], lbuf.at[s, i], l_sem.at[s])
            for i, src in enumerate((bg_hbm, bu_hbm, ad_hbm))
        ]

    x_copy = pltpu.make_async_copy(x_hbm, x_own, misc_sem.at[0])
    bd_copy = pltpu.make_async_copy(bd_hbm, bdbuf, misc_sem.at[1])
    x_copy.start()
    for i in range(2):
        for c in range(n_chunk):
            src = (ag_hbm, au_hbm)[i]
            pltpu.make_async_copy(
                src.at[:, pl.ds(c * SUB, SUB)], abuf.at[c, pl.ds(i * ranks, ranks)], a_sem.at[c]
            ).start()

    barrier = pltpu.get_barrier_semaphore()
    for peer in peers:
        pl.semaphore_signal(barrier, inc=1, device_id={"data": peer}, device_id_type=MESH)

    for i in range(PAIRS):
        issue(i, i)
    for n in range(LBUFS):
        for cp in l_copies(n, n):
            cp.start()
    bd_copy.start()

    ids = ids_ref[...].astype(F32)
    r0 = lax.broadcasted_iota(jnp.int32, (tok, tok), 0).astype(F32)
    r1 = lax.broadcasted_iota(jnp.int32, (tok, tok), 1).astype(F32)
    ids_row = jnp.broadcast_to(ids, (tok, tok))
    ids_col = jnp.broadcast_to(jnp.sum(jnp.where(r0 == r1, ids_row, 0.0), axis=1, keepdims=True), (tok, tok))
    own_row = jnp.floor((ids_row + 0.5) * (1.0 / per_owner))
    own_col = jnp.floor((ids_col + 0.5) * (1.0 / per_owner))
    same = own_row == own_col
    arr_row = jnp.sum(jnp.where(same & (r0 < r1), 1.0, 0.0), axis=0, keepdims=True)
    arr_col = jnp.sum(jnp.where(same & (r1 < r0), 1.0, 0.0), axis=1, keepdims=True)
    slot_row = own_row[:1, :] * cap + arr_row
    slot_col = own_col[:, :1] * cap + arr_col
    loc_col = ids_col[:, :1] - own_col[:, :1] * per_owner
    s_row = lax.broadcasted_iota(jnp.int32, (rows, tok), 0).astype(F32)
    spread = jnp.where(s_row == jnp.broadcast_to(slot_row, (rows, tok)), 1.0, 0.0).astype(BF16)
    s_col = lax.broadcasted_iota(jnp.int32, (tok, rows), 1).astype(F32)
    pick[...] = jnp.where(s_col == jnp.broadcast_to(slot_col, (tok, rows)), 1.0, 0.0).astype(BF16)
    lane = lax.broadcasted_iota(jnp.int32, (tok, ranks), 1).astype(F32)
    lane_ad = jnp.floor((lane + 0.5) * (1.0 / rank))
    mine = jnp.where(lane_ad == jnp.broadcast_to(loc_col, (tok, ranks)), 1.0, 0.0).astype(BF16)

    mask_send[...] = dot(spread, mine).astype(BF16).reshape(mask_send.shape)
    x_copy.wait()
    for c in range(n_chunk):
        part = dot(spread, x_own[:, c * SUB:(c + 1) * SUB]).astype(BF16)
        for q in range(blocks):
            send[:, c * blocks + q] = part[:, q * LANES:(q + 1) * LANES].reshape(groups, per_msg, PACK, LANES)

    mine_at = pl.ds(per_msg * me, per_msg)

    def exchange(src, dst, first, count, send_sem, recv_sem):
        for peer in peers:
            pltpu.make_async_remote_copy(
                src_ref=src.at[peer, pl.ds(first, count)], dst_ref=dst.at[pl.ds(first, count), mine_at],
                send_sem=send_sem, recv_sem=recv_sem, device_id={"data": peer}, device_id_type=MESH,
            ).start()

    def send_out(j):
        exchange(back_send, back_recv, j * blocks, blocks, b_send.at[j], b_recv.at[j])

    def await_peers(buf, first, count, sem):
        view = buf.at[pl.ds(first, count), pl.ds(0, per_msg * (groups - 1))]
        pltpu.make_async_copy(view, view, sem).wait()

    def await_sent(buf, first, count, sem):
        view = buf.at[pl.ds(0, groups - 1), pl.ds(first, count)]
        pltpu.make_async_copy(view, view, sem).wait()

    @pl.loop(0, n_chunk * blocks)
    def _(q):
        recv[q, mine_at] = send[me, q]

    mask_recv[mine_at] = mask_send[mine_at]

    pl.semaphore_wait(barrier, groups - 1)

    for m, (c, count) in enumerate(messages):
        exchange(send, recv, c * blocks, count * blocks, xs_send.at[m], xs_recv.at[m])
    for peer in peers:
        pltpu.make_async_remote_copy(
            src_ref=mask_send.at[pl.ds(per_msg * peer, per_msg)], dst_ref=mask_recv.at[mine_at],
            send_sem=m_send, recv_sem=m_recv, device_id={"data": peer}, device_id_type=MESH,
        ).start()

    def arrive(m):
        first, count = messages[m]
        await_peers(recv, first * blocks, count * blocks, xs_recv.at[m])
        for c in range(first, first + count):
            for q in range(blocks):
                xs[c, :, q * LANES:(q + 1) * LANES] = recv[c * blocks + q].reshape(rows, LANES)
            pltpu.make_async_copy(abuf.at[c], abuf.at[c], a_sem.at[c]).wait()
            part = nt_dot(xs[c], abuf[c])
            low[...] = part if c == 0 else low[...] + part

    def masked(value):
        mask = mask_recv[...].reshape(rows, ranks).astype(F32) > 0.0
        return jnp.where(mask, value.astype(BF16).astype(F32), 0.0).astype(BF16)

    def delta(a, b):
        return (scale * dot(a, b)).astype(BF16).astype(F32)

    def deep(p):
        return jnp.concatenate([xs[2 * p], xs[2 * p + 1]], axis=1)

    def finish(n, s, gate, up):
        pltpu.make_async_copy(lbuf.at[s], lbuf.at[s], l_sem.at[s]).wait()
        for p in range(2):
            cols = slice(p * SUB // 2, (p + 1) * SUB // 2)
            g = gate(cols) + delta(lowm[0], lbuf[s, 0, :, cols])
            u = up(cols) + delta(lowm[1], lbuf[s, 1, :, cols])
            hid[n, :, cols] = (jax.nn.silu(g) * u).astype(BF16)
        lowd[...] += nt_dot(hid[n], lbuf[s, 2])

    at = 0
    for c in range(2):
        arrive(c)

        def shallow(n, slots, c=c):
            wait_w(slots[0])
            for which in range(2):
                for half in range(2):
                    part = dot(xs[c], wbuf[slots[0], which, half * SUB:(half + 1) * SUB])
                    if c == 0:
                        acc[which, 2 * n + half] = part
                    else:
                        acc[which, 2 * n + half] += part

        run(at, HELD, 1, shallow)
        at += HELD

    for p in range(1, n_deep):
        arrive(p + 1)
        last = p == n_deep - 1
        if last:
            view = mask_recv.at[pl.ds(0, per_msg * (groups - 1))]
            pltpu.make_async_copy(view, view, m_recv).wait()
            for i in range(2):
                lowm[i] = masked(low[:, i * ranks:(i + 1) * ranks])
            lowd[...] = jnp.zeros_like(lowd)

        def pair(n2, slots, p=p, last=last):
            for i in range(2):
                n = 2 * n2 + i
                wait_w(slots[i])
                for which in range(2):
                    acc[which, n] += dot(deep(p), wbuf[slots[i], which])
                if last:
                    s = lax.rem(n, LBUFS)
                    finish(n, s, lambda cols: acc[0, n, :, cols], lambda cols: acc[1, n, :, cols])
                    for cp in l_copies(n + LBUFS, s):
                        cp.start()

        run(at, HELD, 2, pair)
        at += n_held

    for with_copies, lo, hi in ((True, n_held, n_tile - LBUFS), (False, n_tile - LBUFS, n_tile)):

        def whole(step, slots, with_copies=with_copies, lo=lo):
            n = lo + step
            for slot in slots:
                wait_w(slot)
            for which in range(2):
                total = dot(deep(0), wbuf[slots[0], which])
                for p in range(1, n_deep):
                    total = total + dot(deep(p), wbuf[slots[p], which])
                acc[which, 0] = total
            s = lax.rem(n, LBUFS)
            finish(n, s, lambda cols: acc[0, 0, :, cols], lambda cols: acc[1, 0, :, cols])
            if with_copies:
                for cp in l_copies(n + LBUFS, s):
                    cp.start()

        run(at, hi - lo, n_deep, whole)
        at += (hi - lo) * n_deep

    lowm[0] = masked(lowd[...])
    bd_copy.wait()

    def combine(j):
        await_peers(back_recv, j * blocks, blocks, b_recv.at[j])
        part = jnp.concatenate([back_recv[j * blocks + q].reshape(rows, LANES) for q in range(blocks)], axis=1)
        o0 = pl.multiple_of(j * SUB, SUB)
        out_own[j] = dot(pick[...], part).astype(BF16)
        pltpu.make_async_copy(out_own.at[j], out_hbm.at[:, pl.ds(o0, SUB)], o_sem).start()

    def column(j, slots):
        cut = (n_kp + 1) // 2
        o0 = pl.multiple_of(j * SUB, SUB)
        for part, (lo, hi) in enumerate(((0, cut), (cut, n_kp))):
            total = None
            for kp in range(lo, hi):
                wait_w(slots[kp])
            for kp in range(lo, hi):
                for half in range(2):
                    h = 4 * kp + 2 * half
                    term = dot(jnp.concatenate([hid[h], hid[h + 1]], axis=1), wbuf[slots[kp], half])
                    total = term if total is None else total + term
            if part == 0:
                oacc[...] = total

                @pl.when(j > 0)
                def _():
                    send_out(j - 1)

                @pl.when(j > 1)
                def _():
                    combine(j - 2)
            else:
                oacc[...] += total
        row = (xs[j].astype(F32) + (oacc[...] + delta(lowm[0], bdbuf[:, pl.ds(o0, SUB)]))).astype(BF16)
        for q in range(blocks):
            back_send[:, j * blocks + q] = row[:, q * LANES:(q + 1) * LANES].reshape(groups, per_msg, PACK, LANES)
        for q in range(blocks):
            back_recv[j * blocks + q, mine_at] = back_send[me, j * blocks + q]

    run(at, n_out, n_kp, column)

    send_out(n_out - 1)
    combine(n_out - 2)
    combine(n_out - 1)

    for m, (c, count) in enumerate(messages):
        await_sent(send, c * blocks, count * blocks, xs_send.at[m])
    view = mask_send.at[pl.ds(0, per_msg * (groups - 1))]
    pltpu.make_async_copy(view, view, m_send).wait()
    for j in range(n_out):
        await_sent(back_send, j * blocks, blocks, b_send.at[j])
    pltpu.make_async_copy(out_own, out_own, o_sem).wait()


def solution(mesh):
    groups = mesh.shape["data"]
    row_spec = P(("rep", "data"), None)
    id_spec = P(("rep", "data"))
    owned_spec = P("data", None, None)

    def device_step(x, adapter_id, w_gate, w_up, w_down, a_gate, b_gate, a_up, b_up, a_down, b_down):
        tok, width = x.shape
        wide = w_gate.shape[1]
        per_owner, rank = a_gate.shape[:2]
        cap = (3 * tok + groups - 1) // groups
        rows, ranks = groups * cap, per_owner * rank
        per_msg, n_chunk, n_tile = cap // PACK, width // SUB, wide // SUB
        assert cap % PACK == 0 and width % (2 * SUB) == 0 and wide % (4 * SUB) == 0 and ranks == LANES

        def flat(m):
            return m.reshape(ranks, m.shape[2])

        vm = pltpu.VMEM
        any_spec = pl.BlockSpec(memory_space=pl.ANY)
        msg = (groups, width // LANES, per_msg, PACK, LANES)
        got = (width // LANES, groups * per_msg, PACK, LANES)
        small = (groups * per_msg, PACK, LANES)
        dma = pltpu.SemaphoreType.DMA
        return pl.pallas_call(
            functools.partial(layer_kernel, groups, cap, ALPHA / rank, per_owner, rank),
            out_shape=jax.ShapeDtypeStruct((tok, width), BF16),
            in_specs=[any_spec, pl.BlockSpec(memory_space=pltpu.VMEM)] + [any_spec] * 9,
            out_specs=any_spec,
            scratch_shapes=[
                vm((tok, width), BF16), vm(msg, BF16), vm(small, BF16), vm(got, BF16), vm(small, BF16),
                vm((n_chunk, rows, SUB), BF16), vm((2, 2 * HELD, rows, SUB), F32), vm((n_tile, rows, SUB), BF16),
                vm((PAIRS, 2, 2 * SUB, SUB), BF16), vm((n_chunk, 2 * ranks, SUB), BF16),
                vm((LBUFS, 3, ranks, SUB), BF16),
                vm((ranks, width), BF16), vm((rows, 2 * ranks), F32), vm((2, rows, ranks), BF16),
                vm((rows, ranks), F32), vm((rows, SUB), F32), vm(msg, BF16), vm(got, BF16),
                vm((width // SUB, tok, SUB), BF16), vm((tok, rows), BF16),
                dma((PAIRS,)), dma((2,)), dma((n_chunk,)), dma((LBUFS,)), dma((n_chunk,)), dma((n_chunk,)), dma, dma,
                dma((width // SUB,)), dma((width // SUB,)), dma,
            ],
            compiler_params=pltpu.CompilerParams(
                collective_id=0, has_side_effects=True, vmem_limit_bytes=67043328),
            name="owner_layer",
        )(x, adapter_id.reshape(1, tok), w_gate, w_up, w_down, flat(a_gate), flat(b_gate), flat(a_up), flat(b_up),
          flat(a_down), flat(b_down))

    return jax.shard_map(
        device_step, mesh=mesh,
        in_specs=(row_spec, id_spec, P(), P(), P()) + (owned_spec,) * 6,
        out_specs=row_spec, check_vma=False)
```

time: 183 us -> 147 us (0.80)
  Pallas kernels: 181 us -> 145 us
    pallas_call x1, Pallas kernels: 181 us -> 145 us  [device_step(): pl.pallas_call(functools.partial(layer_kernel, groups, cap, ALPHA / rank,...]
where the time goes in v2:
time: 147 us
  Pallas kernels  145 us (99%)
  local copies, waits for them, and re-layouts  1.87 us (1%)
    pallas_call x1, Pallas kernels, device_step(): pl.pallas_call(functools.partial(layer_kernel, groups, cap, ALPHA / rank,...  145 us

profile of v2, /device:TPU:21, one launch (start us, length us, event | category | flops | bytes accessed | tf_op | source)
XLA Modules:
  0.0 147.2 jit_solution(17491841967164365183)
XLA Ops:
  0.0 145.4 %owner_layer.1 = bf16[64,4096]{1,0:T(8,128)(2,1)} custom-call(bf16[64,4096]{1,0:T(8,128)(2,1)} %x_hbm.1, s32[1,64]{1,0:T(1,128)} %bitcast.13, bf16[4096,14336]{1,0:T(8,128)(2,1)} %wg_hbm.1, bf16[4096,14336]{1,0:T(8,128)(2,1)} %wu_hbm.1, bf16[14336,4096]{1,0:T(8,128)(2,1)} %wd_hbm.1, bf16[128,4096]{1,0:T(8,128)(2,1)} %bitcast.10, bf16[128,14336]{1,0:T(8,128)(2,1)} %bitcast.7, ...), custom_call_target="tpu_custom_call" | custom-call | tf_op jit(solution)/shard_map/owner_layer/pallas_call | solution.py:419
  145.4 1.9 %copy.13 = bf16[64,4096]{1,0:T(8,128)(2,1)} copy(bf16[64,4096]{1,0:T(8,128)(2,1)} %owner_layer.1) | data formatting | bytes 1048576

commit v3 on v2

--- a/solution.py
+++ b/solution.py
@@ -16,6 +16,8 @@
 HELD = 9
 PAIRS = 12
 LBUFS = 4
+LAG = 5
+STEP = 3
 
 
 def nt_dot(a, b):
@@ -58,6 +60,10 @@
     seen += [off for off in range(1, groups) if off not in seen]
     peers = [lax.rem(me + off, groups) for off in seen]
 
+    barrier = pltpu.get_barrier_semaphore()
+    for peer in peers:
+        pl.semaphore_signal(barrier, inc=1, device_id={"data": peer}, device_id_type=MESH)
+
     def nxt(slot):
         return jnp.where(slot == PAIRS - 1, 0, slot + 1)
 
@@ -87,71 +93,69 @@
     def wait_w(slot):
         pltpu.make_async_copy(wbuf.at[slot], wbuf.at[slot], w_sem.at[slot]).wait()
 
-    def issue(i, slot):
-        for count, start in (
-            (2 * HELD, lambda i: start_a1(slot, i // HELD, i % HELD)),
-            ((n_deep - 1) * n_held, lambda i: start_gu(slot, 1 + i // n_held, i % n_held)),
-            ((n_tile - n_held) * n_deep, lambda i: start_gu(slot, i % n_deep, n_held + i // n_deep)),
-            (n_out * n_kp, lambda i: start_d(slot, i // n_kp, i % n_kp)),
-        ):
-            if i < count:
-                start(i)
-                return
-            i -= count
-
     kinds = []
     for o in range(2):
         kinds += [("a1", o, n) for n in range(HELD)]
     for o in range(1, n_deep):
         kinds += [("gu", o, n) for n in range(n_held)]
     for n in range(n_held, n_tile):
-        kinds += [("gu", o, n) for o in range(n_deep)]
+        kinds += [("gb", n, o) for o in range(n_deep)]
     for o in range(n_out):
         kinds += [("d", o, n) for n in range(n_kp)]
-    starts = {"a1": start_a1, "gu": start_gu, "d": start_d}
+    starts = {"a1": start_a1, "gu": start_gu, "gb": lambda slot, n, o: start_gu(slot, o, n), "d": start_d}
+    inner = {"a1": HELD, "gu": n_held, "gb": n_deep, "d": n_kp}
     n_pair = len(kinds)
 
     def run(first, count, size, body):
+        def ahead(step):
+            items = [kinds[q] for q in range(first + step * size + PAIRS, first + (step + 1) * size + PAIRS)
+                     if q < n_pair]
+            return {k for k, _, _ in items}, items
+
         step = 0
         while step < count:
-            def refill(s):
-                return [kinds[q] if q < n_pair else None for q in
-                        range(first + s * size + PAIRS, first + (s + 1) * size + PAIRS)]
-
-            def rule(a, b):
-                if any((p is None) != (q is None) or (p and p[0] != q[0]) for p, q in zip(a, b)):
-                    return None
-                return [p and (q[1] - p[1], q[2] - p[2]) for p, q in zip(a, b)]
-
+            names, items = ahead(step)
             end = step + 1
-            delta = None
-            while end < count:
-                d = rule(refill(end - 1), refill(end))
-                if d is None or (delta is not None and d != delta):
-                    break
-                delta = d
-                end += 1
-            base = refill(step)
-            slot0 = (first + step * size) % PAIRS
-
-            def one(s, slot, base=base, delta=delta, step=step):
+            if len(names) == 1:
+                while end < count and (ahead(end)[0] == names or (names == {"d"} and not ahead(end)[0])):
+                    end += 1
+            guarded = names == {"d"}
+
+            def one(s, carry, items=items, names=names, guarded=guarded, looped=end - step > 1):
+                slot, o, n = carry
                 slots = [slot]
                 for _ in range(size - 1):
                     slots.append(nxt(slots[-1]))
-                body(s, slots)
-                for i, item in enumerate(base):
-                    if item is None:
-                        continue
-                    kind, o, n = item
-                    if delta is not None:
-                        o, n = o + (s - step) * delta[i][0], n + (s - step) * delta[i][1]
-                    starts[kind](slots[i], o, n)
-                return nxt(slots[-1])
-
+                todo = []
+                if looped:
+                    kind = items[0][0]
+                    for _ in range(size):
+                        todo.append((kind, o, n))
+                        wrap = n == inner[kind] - 1
+                        o, n = jnp.where(wrap, o + 1, o), jnp.where(wrap, 0, n + 1)
+                else:
+                    todo = items
+
+                def refill(i):
+                    if i >= len(todo):
+                        return
+                    kind, oo, nn = todo[i]
+                    if looped and guarded:
+                        @pl.when(oo < n_out)
+                        def _():
+                            starts[kind](slots[i], oo, nn)
+                    else:
+                        starts[kind](slots[i], oo, nn)
+
+                body(s, slots, refill)
+                return nxt(slots[-1]), o, n
+
+            slot0 = (first + step * size) % PAIRS
+            _, o0, n0 = items[0] if items else (None, 0, 0)
             if end - step == 1:
-                one(step, slot0)
+                one(step, (jnp.int32(slot0), 0, 0))
             else:
-                lax.fori_loop(step, end, one, jnp.int32(slot0))
+                lax.fori_loop(step, end, one, (jnp.int32(slot0), jnp.int32(o0), jnp.int32(n0)))
             step = end
 
     def l_copies(n, s):
@@ -171,16 +175,6 @@
                 src.at[:, pl.ds(c * SUB, SUB)], abuf.at[c, pl.ds(i * ranks, ranks)], a_sem.at[c]
             ).start()
 
-    barrier = pltpu.get_barrier_semaphore()
-    for peer in peers:
-        pl.semaphore_signal(barrier, inc=1, device_id={"data": peer}, device_id_type=MESH)
-
-    for i in range(PAIRS):
-        issue(i, i)
-    for n in range(LBUFS):
-        for cp in l_copies(n, n):
-            cp.start()
-    bd_copy.start()
 
     ids = ids_ref[...].astype(F32)
     r0 = lax.broadcasted_iota(jnp.int32, (tok, tok), 0).astype(F32)
@@ -246,6 +240,13 @@
             send_sem=m_send, recv_sem=m_recv, device_id={"data": peer}, device_id_type=MESH,
         ).start()
 
+    for i in range(PAIRS):
+        starts[kinds[i][0]](i, kinds[i][1], kinds[i][2])
+    for n in range(LBUFS):
+        for cp in l_copies(n, n):
+            cp.start()
+    bd_copy.start()
+
     def arrive(m):
         first, count = messages[m]
         await_peers(recv, first * blocks, count * blocks, xs_recv.at[m])
@@ -266,35 +267,48 @@
     def deep(p):
         return jnp.concatenate([xs[2 * p], xs[2 * p + 1]], axis=1)
 
-    def finish(n, s, gate, up):
+    def l_wait(s):
         pltpu.make_async_copy(lbuf.at[s], lbuf.at[s], l_sem.at[s]).wait()
+
+    def finish(n, s, base):
         for p in range(2):
             cols = slice(p * SUB // 2, (p + 1) * SUB // 2)
-            g = gate(cols) + delta(lowm[0], lbuf[s, 0, :, cols])
-            u = up(cols) + delta(lowm[1], lbuf[s, 1, :, cols])
+            g = base(0, cols) + delta(lowm[0], lbuf[s, 0, :, cols])
+            u = base(1, cols) + delta(lowm[1], lbuf[s, 1, :, cols])
             hid[n, :, cols] = (jax.nn.silu(g) * u).astype(BF16)
         lowd[...] += nt_dot(hid[n], lbuf[s, 2])
+
+    def l_next(n, s):
+        @pl.when(n + LBUFS < n_tile)
+        def _():
+            for cp in l_copies(n + LBUFS, s):
+                cp.start()
 
     at = 0
     for c in range(2):
         arrive(c)
 
-        def shallow(n, slots, c=c):
-            wait_w(slots[0])
-            for which in range(2):
-                for half in range(2):
-                    part = dot(xs[c], wbuf[slots[0], which, half * SUB:(half + 1) * SUB])
-                    if c == 0:
-                        acc[which, 2 * n + half] = part
-                    else:
-                        acc[which, 2 * n + half] += part
-
-        run(at, HELD, 1, shallow)
+        def shallow(step, slots, refill, c=c):
+            for slot in slots:
+                wait_w(slot)
+            for i, slot in enumerate(slots):
+                for which in range(2):
+                    for half in range(2):
+                        part = dot(xs[c], wbuf[slot, which, half * SUB:(half + 1) * SUB])
+                        n = 2 * (len(slots) * step + i) + half
+                        if c == 0:
+                            acc[which, n] = part
+                        else:
+                            acc[which, n] += part
+                refill(i)
+
+        run(at, HELD // STEP, STEP, shallow)
         at += HELD
 
     for p in range(1, n_deep):
         arrive(p + 1)
         last = p == n_deep - 1
+        size = 2 if last else STEP
         if last:
             view = mask_recv.at[pl.ds(0, per_msg * (groups - 1))]
             pltpu.make_async_copy(view, view, m_recv).wait()
@@ -302,40 +316,45 @@
                 lowm[i] = masked(low[:, i * ranks:(i + 1) * ranks])
             lowd[...] = jnp.zeros_like(lowd)
 
-        def pair(n2, slots, p=p, last=last):
-            for i in range(2):
-                n = 2 * n2 + i
-                wait_w(slots[i])
-                for which in range(2):
-                    acc[which, n] += dot(deep(p), wbuf[slots[i], which])
+        def some(step, slots, refill, p=p, last=last):
+            for i, slot in enumerate(slots):
+                wait_w(slot)
+                if last:
+                    l_wait(lax.rem(len(slots) * step + i, LBUFS))
+            for i, slot in enumerate(slots):
+                n = len(slots) * step + i
                 if last:
                     s = lax.rem(n, LBUFS)
-                    finish(n, s, lambda cols: acc[0, n, :, cols], lambda cols: acc[1, n, :, cols])
-                    for cp in l_copies(n + LBUFS, s):
-                        cp.start()
-
-        run(at, HELD, 2, pair)
+                    finish(n, s, lambda which, cols: acc[which, n, :, cols] + dot(deep(p), wbuf[slot, which, :, cols]))
+                    l_next(n, s)
+                else:
+                    for which in range(2):
+                        acc[which, n] += dot(deep(p), wbuf[slot, which])
+                refill(i)
+
+        run(at, n_held // size, size, some)
         at += n_held
 
-    for with_copies, lo, hi in ((True, n_held, n_tile - LBUFS), (False, n_tile - LBUFS, n_tile)):
-
-        def whole(step, slots, with_copies=with_copies, lo=lo):
-            n = lo + step
-            for slot in slots:
-                wait_w(slot)
-            for which in range(2):
-                total = dot(deep(0), wbuf[slots[0], which])
-                for p in range(1, n_deep):
-                    total = total + dot(deep(p), wbuf[slots[p], which])
-                acc[which, 0] = total
-            s = lax.rem(n, LBUFS)
-            finish(n, s, lambda cols: acc[0, 0, :, cols], lambda cols: acc[1, 0, :, cols])
-            if with_copies:
-                for cp in l_copies(n + LBUFS, s):
-                    cp.start()
-
-        run(at, hi - lo, n_deep, whole)
-        at += (hi - lo) * n_deep
+    def whole(step, slots, refill):
+        n = n_held + step
+        s = lax.rem(n, LBUFS)
+        for slot in slots:
+            wait_w(slot)
+        l_wait(s)
+
+        def base(which, cols):
+            total = dot(deep(0), wbuf[slots[0], which, :, cols])
+            for p in range(1, n_deep):
+                total = total + dot(deep(p), wbuf[slots[p], which, :, cols])
+            return total
+
+        finish(n, s, base)
+        for i in range(len(slots)):
+            refill(i)
+        l_next(n, s)
+
+    run(at, n_tile - n_held, n_deep, whole)
+    at += (n_tile - n_held) * n_deep
 
     lowm[0] = masked(lowd[...])
     bd_copy.wait()
@@ -347,7 +366,15 @@
         out_own[j] = dot(pick[...], part).astype(BF16)
         pltpu.make_async_copy(out_own.at[j], out_hbm.at[:, pl.ds(o0, SUB)], o_sem).start()
 
-    def column(j, slots):
+    def column(j, slots, refill):
+        @pl.when(j > 0)
+        def _():
+            send_out(j - 1)
+
+        @pl.when(j >= LAG)
+        def _():
+            combine(j - LAG)
+
         cut = (n_kp + 1) // 2
         o0 = pl.multiple_of(j * SUB, SUB)
         for part, (lo, hi) in enumerate(((0, cut), (cut, n_kp))):
@@ -361,27 +388,24 @@
                     total = term if total is None else total + term
             if part == 0:
                 oacc[...] = total
-
-                @pl.when(j > 0)
-                def _():
-                    send_out(j - 1)
-
-                @pl.when(j > 1)
-                def _():
-                    combine(j - 2)
             else:
-                oacc[...] += total
-        row = (xs[j].astype(F32) + (oacc[...] + delta(lowm[0], bdbuf[:, pl.ds(o0, SUB)]))).astype(BF16)
-        for q in range(blocks):
-            back_send[:, j * blocks + q] = row[:, q * LANES:(q + 1) * LANES].reshape(groups, per_msg, PACK, LANES)
+                total = oacc[...] + total + delta(lowm[0], bdbuf[:, pl.ds(o0, SUB)])
+                row = (xs[j].astype(F32) + total).astype(BF16)
+                for q in range(blocks):
+                    back_send[:, j * blocks + q] = row[:, q * LANES:(q + 1) * LANES].reshape(
+                        groups, per_msg, PACK, LANES)
+            for kp in range(lo, hi):
+                refill(kp)
         for q in range(blocks):
             back_recv[j * blocks + q, mine_at] = back_send[me, j * blocks + q]
 
     run(at, n_out, n_kp, column)
 
     send_out(n_out - 1)
-    combine(n_out - 2)
-    combine(n_out - 1)
+
+    @pl.loop(n_out - LAG, n_out)
+    def _(j):
+        combine(j)
 
     for m, (c, count) in enumerate(messages):
         await_sent(send, c * blocks, count * blocks, xs_send.at[m])

time: 147 us -> 134 us (0.912)
  Pallas kernels: 145 us -> 132 us
    pallas_call x1, Pallas kernels: 145 us -> 132 us  [device_step(): pl.pallas_call(functools.partial(layer_kernel, groups, cap, ALPHA / rank,...]
where the time goes in v3:
time: 134 us
  Pallas kernels  132 us (99%)
  local copies, waits for them, and re-layouts  1.87 us (1%)
    pallas_call x1, Pallas kernels, device_step(): pl.pallas_call(functools.partial(layer_kernel, groups, cap, ALPHA / rank,...  132 us

profile of v3, /device:TPU:21, one launch (start us, length us, event | category | flops | bytes accessed | tf_op | source)
XLA Modules:
  0.0 133.6 jit_solution(756177528047604564)
XLA Ops:
  0.0 131.7 %owner_layer.1 = bf16[64,4096]{1,0:T(8,128)(2,1)} custom-call(bf16[64,4096]{1,0:T(8,128)(2,1)} %x_hbm.1, s32[1,64]{1,0:T(1,128)} %bitcast.13, bf16[4096,14336]{1,0:T(8,128)(2,1)} %wg_hbm.1, bf16[4096,14336]{1,0:T(8,128)(2,1)} %wu_hbm.1, bf16[14336,4096]{1,0:T(8,128)(2,1)} %wd_hbm.1, bf16[128,4096]{1,0:T(8,128)(2,1)} %bitcast.10, bf16[128,14336]{1,0:T(8,128)(2,1)} %bitcast.7, ...), custom_call_target="tpu_custom_call" | custom-call | tf_op jit(solution)/shard_map/owner_layer/pallas_call | solution.py:443
  131.7 1.9 %copy.13 = bf16[64,4096]{1,0:T(8,128)(2,1)} copy(bf16[64,4096]{1,0:T(8,128)(2,1)} %owner_layer.1) | data formatting | bytes 1048576
